TPU v7x, 256 devices: a whole 4x4x8 slice. The times are simulated.
256 devices in a mesh: seq: 16 (over z, core), head: 4 (over x), batch: 4 (over y).
Axes of the slice: x: 4, y: 4, z: 8, core: 2. Of those that a mesh axis runs over, the one named last changes fastest.
Arguments:
- queries: bfloat16 [4, 8192, 8, 8, 128], P('batch', 'seq', 'head'), may hold values from -160 to 160
- key_rows: bfloat16 [4, 8192, 8, 128], P('batch', 'seq'), may hold values from -6 to 6
- value_rows: bfloat16 [4, 8192, 8, 128], P('batch', 'seq'), may hold values from -6 to 6
- compressed: bfloat16 [4, 128, 8, 128], P('batch', 'seq'), may hold values from -6 to 6
- chosen: int32 [4, 128, 8, 16], P('batch', 'seq'), may hold values from 0 to 127, as said below
Outputs:
- block_scores: float32 [4, 128, 8, 128], P('batch', 'seq', 'head')
- attended: bfloat16 [4, 8192, 8, 8, 128], P('batch', 'seq', 'head')
Inputs may be any that keep to these rules, and one draw needn't show every extreme that they name: `chosen`: every entry is at most its own tile number, and entry 0 of every row is the tile's own block. Over the tiles of one device of seq and one group, at most 2 different blocks of any other device are named, and every device after the first names exactly 2 blocks of the first device for each group.
All inputs are finite; a program needn't handle non-finite values.
Results may differ from a plain program's by a relative error of at most 0.008.
Values may be sent and summed in bfloat16 or wider, within the bound.
No kernel may reach another device: no remote copies, remote signals or barrier semaphores. Data moves between devices by JAX's collectives and lax.ppermute only.
A program may use at most 128 MiB of HBM per device.

v0:
```python
import jax
import jax.numpy as jnp
from jax import lax
from jax.sharding import PartitionSpec as P

HPG = 8
BLOCK = 64
TOPN = 16
CAP = 2


def laid_out(blocks, dim):
    dims = list(blocks.shape[1:])
    dims[dim] *= blocks.shape[0]
    return jnp.moveaxis(blocks, 0, dim).reshape(dims)


def copy_for_each(value, axis):
    count = lax.axis_size(axis)
    return lax.all_to_all(
        jnp.broadcast_to(value[None], (count, *value.shape)), axis, 0, 0, tiled=True
    )


def gather_directly(value, axis, dim):
    return laid_out(copy_for_each(value, axis), dim)


def cut_along(value, dim, count):
    dims = value.shape
    blocks = value.reshape(*dims[:dim], count, dims[dim] // count, *dims[dim + 1 :])
    return jnp.moveaxis(blocks, dim, 0)


def sum_at_owner(value, axis, dim):
    count = lax.axis_size(axis)
    blocks = lax.all_to_all(cut_along(value, dim, count), axis, 0, 0, tiled=True)
    return jnp.sum(blocks.astype(jnp.float32), axis=0)


def softmax_parts(scores):
    row_top = jnp.max(scores, axis=-1, keepdims=True)
    weights = jnp.exp(scores - row_top)
    return (weights, jnp.sum(weights, axis=-1, keepdims=True))


def local(queries, key_rows, value_rows, compressed, chosen):
    _, tok_rows, heads_local, groups, head_width = queries.shape
    block_len = BLOCK
    shards = lax.axis_size("seq")
    seq_rank = lax.axis_index("seq")
    blk_dev = tok_rows // block_len
    nblk = blk_dev * shards
    score_scale = head_width ** (-0.5)
    query_rows = queries[0]
    query_pos = seq_rank * tok_rows + jnp.arange(tok_rows, dtype=jnp.int32)
    logits = (
        jnp.einsum(
            "tjgd,ngd->tjgn",
            query_rows,
            gather_directly(compressed, "seq", 1)[0],
            preferred_element_type=jnp.float32,
        )
        * score_scale
    )
    all_blocks = jnp.arange(nblk, dtype=jnp.int32)
    seen = all_blocks[None, :] <= (query_pos // block_len)[:, None]
    logits = jnp.where(seen[:, None, None, :], logits, -jnp.inf)
    weights, totals = softmax_parts(logits)
    probability = weights / totals
    pooled = jnp.sum(
        probability.reshape(blk_dev, block_len, heads_local, groups, nblk), axis=(1, 2)
    )[None]
    shared = sum_at_owner(pooled.astype(jnp.bfloat16), "head", 2)
    tile_ids = seq_rank * blk_dev + jnp.arange(blk_dev, dtype=jnp.int32)
    factor = (tile_ids + 1).astype(jnp.float32) / (block_len * HPG)
    block_scores = shared * factor[None, :, None, None]
    pick_rows = chosen[0]
    onehot = pick_rows[..., None] == all_blocks
    needed = jnp.any(onehot, axis=(0, 2))
    owner_of = all_blocks // blk_dev
    needed = needed & (owner_of != seq_rank)[None, :]
    needed_grid = needed.reshape(groups, shards, blk_dev).astype(jnp.int32)
    rank_in = jnp.cumsum(needed_grid, axis=2) - needed_grid
    places = jnp.arange(CAP, dtype=jnp.int32)
    within = jnp.arange(blk_dev, dtype=jnp.int32)
    matched = (needed_grid[..., None] == 1) & (rank_in[..., None] == places)
    wanted = jnp.sum(jnp.where(matched, within[:, None], 0), axis=2)
    slot_of = blk_dev + owner_of[None, :] * CAP + rank_in.reshape(groups, nblk)
    slot_of = jnp.where(
        owner_of[None, :] == seq_rank, all_blocks[None, :] - seq_rank * blk_dev, slot_of
    )
    pool_index = jnp.sum(jnp.where(onehot, slot_of[None, :, None, :], 0), axis=3)
    key_local = key_rows[0].reshape(blk_dev, block_len, groups, head_width)
    value_local = value_rows[0].reshape(blk_dev, block_len, groups, head_width)
    group_count = groups // lax.axis_size("head")
    group_start = lax.axis_index("head") * group_count
    asked_ids = lax.dynamic_slice_in_dim(wanted, group_start, group_count, 0)
    requested = lax.all_to_all(asked_ids, "seq", split_axis=1, concat_axis=1, tiled=True)
    group_ids = group_start + jnp.arange(requested.shape[0], dtype=jnp.int32)[:, None, None]
    found = jnp.concatenate(
        [key_local[requested, :, group_ids, :], value_local[requested, :, group_ids, :]], axis=-1
    )
    fetched = lax.all_to_all(found, "seq", split_axis=1, concat_axis=1, tiled=True)
    fetched = lax.all_gather(fetched, "head", axis=0, tiled=True)
    key_remote = fetched[..., :head_width].reshape(groups, shards * CAP, block_len, head_width)
    value_remote = fetched[..., head_width:].reshape(groups, shards * CAP, block_len, head_width)
    key_pool = jnp.concatenate([jnp.transpose(key_local, (2, 0, 1, 3)), key_remote], axis=1)
    value_pool = jnp.concatenate([jnp.transpose(value_local, (2, 0, 1, 3)), value_remote], axis=1)
    tile_step = 2
    rounds = blk_dev // tile_step
    group_sel = jnp.arange(groups, dtype=jnp.int32)[None, :, None]

    def attend(inputs):
        query_part, index_part, pick_part, pos_part = inputs
        key_sel = key_pool[group_sel, index_part].reshape(
            tile_step, groups, TOPN * block_len, head_width
        )
        value_sel = value_pool[group_sel, index_part].reshape(
            tile_step, groups, TOPN * block_len, head_width
        )
        key_pos = (
            pick_part[..., None] * block_len + jnp.arange(block_len, dtype=jnp.int32)
        ).reshape(tile_step, groups, TOPN * block_len)
        scores = (
            jnp.einsum("tqhgd,tgkd->tghqk", query_part, key_sel, preferred_element_type=jnp.float32)
            * score_scale
        )
        visible = key_pos[:, :, None, None, :] <= pos_part[:, None, None, :, None]
        scores = jnp.where(visible, scores, -jnp.inf)
        weights, totals = softmax_parts(scores)
        rounded = weights.astype(jnp.bfloat16)
        mixed = jnp.einsum(
            "tghqk,tgkd->tqhgd", rounded, value_sel, preferred_element_type=jnp.float32
        )
        return (mixed / jnp.transpose(totals, (0, 3, 2, 1, 4))).astype(jnp.bfloat16)

    attended = lax.map(
        attend,
        (
            query_rows.reshape(rounds, tile_step, block_len, heads_local, groups, head_width),
            pool_index.reshape(rounds, tile_step, groups, TOPN),
            pick_rows.reshape(rounds, tile_step, groups, TOPN),
            query_pos.reshape(rounds, tile_step, block_len),
        ),
    )
    attended = attended.reshape(1, tok_rows, heads_local, groups, head_width)
    return (block_scores, attended)


def solution(mesh):
    placed = (
        P("batch", "seq", "head", None, None),
        P("batch", "seq", None, None),
        P("batch", "seq", None, None),
        P("batch", "seq", None, None),
        P("batch", "seq", None, None),
    )
    return jax.shard_map(
        local,
        mesh=mesh,
        in_specs=placed,
        out_specs=(P("batch", "seq", "head", None), P("batch", "seq", "head", None, None)),
        check_vma=False,
    )
```

profile of v0, /device:TPU:1, one launch (start us, length us, event | category | flops | bytes accessed | tf_op | source)
XLA Modules:
  0.0 301.6 jit_solution(489733168469807748)
XLA Ops:
  10.6 10.0 %all-to-all-start.2 = ((s32[2,16,2]{2,0,1:T(2,128)}), s32[2,16,2]{2,0,1:T(2,128)S(1)}, u32[]{:S(2)}, u32[]{:S(2)}) async-start(s32[2,16,2]{2,0,1:T(2,128)} %copy.67), calls=%async_computation.2 | async-start | bytes 32768 | tf_op jit(solution)/shard_map/all_to_all | solution.py:99
  23.3 4.5 %all-to-all-done.2 = s32[2,16,2]{2,0,1:T(2,128)S(1)} async-done(((s32[2,16,2]{2,0,1:T(2,128)}), s32[2,16,2]{2,0,1:T(2,128)S(1)}, u32[]{:S(2)}, u32[]{:S(2)}) %all-to-all-start.2) | async-done | bytes 288 | tf_op jit(solution)/shard_map/all_to_all | solution.py:99
  32.6 53.9 %all_to_all.20 = bf16[2,16,2,64,256]{4,3,2,0,1:T(8,128)(2,1)S(1)} all-to-all(bf16[2,16,2,64,256]{4,3,2,0,1:T(8,128)(2,1)S(1)} %copy.70), channel_id=1, replica_groups=mesh['seq'=16,'head'=4,'batch'=4] {'seq'}, dimensions={1} | all-to-all | bytes 4194304 | tf_op jit(solution)/shard_map/all_to_all | solution.py:104
  94.3 8.8 %all-to-all-done = bf16[16,1,8,8,128]{4,2,3,1,0:T(8,128)(2,1)S(1)} async-done(((bf16[16,1,8,8,128]{4,2,3,1,0:T(8,128)(2,1)}), bf16[16,1,8,8,128]{4,2,3,1,0:T(8,128)(2,1)S(1)}, u32[]{:S(2)}, u32[]{:S(2)}) %all-to-all-start) | async-done | bytes 262176 | tf_op jit(solution)/shard_map/all_to_all | solution.py:20
  106.5 7.5 %fusion.27 = f32[512,2,8,128]{0,3,1,2:T(8,128)} fusion(f32[8,128,512,2]{2,1,3,0:T(8,128)} %fusion.30, pred[512,128]{0,1:T(8,128)(4,1)} %iota_compare_fusion.1), kind=kOutput, calls=%fused_computation.35 | output fusion | flops 5259518 | bytes 8454144 | tf_op jit(solution)/shard_map/div | solution.py:70
  114.1 8.2 %divide_reduce_fusion = f32[512,8,128]{0,2,1:T(8,128)} fusion(f32[512,2,8,128]{0,3,1,2:T(8,128)} %fusion.27, f32[8,128,512,2]{2,1,3,0:T(8,128)} %fusion.30, pred[512,128]{0,1:T(8,128)(4,1)S(1)} %copy-done.5), kind=kOutput, calls=%fused_computation.40 | output fusion | flops 6824063 | bytes 10551296 | tf_op jit(solution)/shard_map/sub | solution.py:43
  131.6 4.6 %all-to-all-done.1 = bf16[4,1,8,2,128]{4,3,2,1,0:T(2,128)(2,1)S(1)} async-done(((bf16[4,1,8,2,128]{4,3,2,1,0:T(2,128)(2,1)}), bf16[4,1,8,2,128]{4,3,2,1,0:T(2,128)(2,1)S(1)}, u32[]{:S(2)}, u32[]{:S(2)}) %all-to-all-start.1) | async-done | bytes 16416 | tf_op jit(solution)/shard_map/all_to_all | solution.py:37
  136.9 33.6 %all-gather.2.cloned.1.call-done = bf16[8,16,2,64,256]{4,3,2,1,0:T(8,128)(2,1)} async-done(((bf16[2,16,2,64,256]{4,3,2,1,0:T(8,128)(2,1)}), bf16[8,16,2,64,256]{4,3,2,1,0:T(8,128)(2,1)}) %all-gather.2.cloned.1.call-update) | async-done | bytes 8388624 | tf_op jit(solution)/shard_map/all_gather | solution.py:105
  170.5 4.5 %fusion.56 = (bf16[8,16,2,64,128]{4,3,2,1,0:T(8,128)(2,1)S(1)}, bf16[8,16,2,64,128]{4,3,2,1,0:T(8,128)(2,1)S(1)}) fusion(bf16[8,16,2,64,256]{4,3,2,1,0:T(8,128)(2,1)} %all-gather.2.cloned.1.call-done), kind=kLoop, calls=%fused_computation.102 | loop fusion | bytes 16777216 | tf_op jit(solution)/shard_map/slice | solution.py:106
  175.0 5.5 %pad_maximum_fusion = (bf16[8,40,64,128]{3,2,1,0:T(8,128)(2,1)}, bf16[8,40,64,128]{3,2,1,0:T(8,128)(2,1)}) fusion(bf16[8,32,64,128]{3,2,1,0:T(8,128)(2,1)S(1)} %bitcast.140, bf16[8,8,64,128]{3,2,1,0:T(8,128)(2,1)S(1)} %bitcast.146, bf16[8,32,64,128]{3,2,1,0:T(8,128)(2,1)S(1)} %bitcast.139, bf16[8,8,64,128]{3,2,1,0:T(8,128)(2,1)S(1)} %bitcast.144), kind=kLoop, calls=%fused_computation.37 | loop fusion | flops 5242880 | bytes 20971520 | tf_op jit(solution)/shard_map/concatenate | solution.py:109
  180.5 114.3 %while.11 = (s32[]{:T(128)}, bf16[4,2,64,2,8,128]{5,4,3,2,1,0:T(8,128)(2,1)}, s32[4,2,8,16]{3,2,1,0:T(8,128)S(1)}, bf16[8,40,64,128]{3,2,1,0:T(8,128)(2,1)}, s32...) while((s32[]{:T(128)}, ...), condition=%wide.region_12.13_spmd.clone, body=%wide.region_9.12_spmd.clone.sunk | while | flops 1098397440 | bytes 91690184 | solution.py:138
  181.6 5.8 %gather_fusion.1 = bf16[256,64,128]{2,1,0:T(8,128)(2,1)} fusion(bf16[8,40,64,128]{3,2,1,0:T(8,128)(2,1)} %get-tuple-element.213, s32[256]{0:T(256)S(1)} %reshape.360), kind=kCustom, calls=%fused_computation.1.clone.clone.1 | custom fusion | bytes 8390656 | tf_op jit(solution)/shard_map/while/body/eval_jaxpr/gather | solution.py:116
  194.7 5.9 %gather_fusion = bf16[256,64,128]{2,1,0:T(8,128)(2,1)} fusion(bf16[8,40,64,128]{3,2,1,0:T(8,128)(2,1)} %get-tuple-element.210, s32[256]{0:T(256)S(1)} %reshape.360), kind=kCustom, calls=%fused_computation.clone.clone.1 | custom fusion | bytes 8390656 | tf_op jit(solution)/shard_map/while/body/eval_jaxpr/gather | solution.py:119
  200.6 7.3 %fusion.76 = bf16[1,2,64,2,8,128]{5,2,3,4,1,0:T(8,128)(2,1)S(1)} fusion(bf16[2,8,1024,128,1]{3,2,4,1,0:T(8,128)(2,1)} %bitcast.137, f32[2,8,1024,64,2]{2,3,4,1,0:T(8,128)} %copy-done, f32[2,8,2,64]{3,2,1,0:T(2,128)S(1)} %get-tuple-element.188, pred[2,8,64,1024]{3,2,1,0:T(8,128)(4,1)S(1)} %broadcast_compare_fusion.4, f32[2,64,2,8]{1,2,3,0:T(2,128)S(1)} %bitcast.149), kind=kOutput, calls=%fused_computation.18.clone.1 | convolution fusion | flops 545783808 | bytes 14172160 | tf_op jit(solution)/shard_map/while/body/eval_jaxpr/tghqk,tgkd->tqhgd/dot_general | solution.py:133
  210.2 5.8 %gather_fusion.1 = bf16[256,64,128]{2,1,0:T(8,128)(2,1)} fusion(bf16[8,40,64,128]{3,2,1,0:T(8,128)(2,1)} %get-tuple-element.213, s32[256]{0:T(256)S(1)} %reshape.360), kind=kCustom, calls=%fused_computation.1.clone.clone.1 | custom fusion | bytes 8390656 | tf_op jit(solution)/shard_map/while/body/eval_jaxpr/gather | solution.py:116
  216.0 4.1 %fusion.74 = (f32[2,8,2,64]{3,2,1,0:T(2,128)S(1)}, f32[2,8,1024,64,2]{2,3,4,1,0:T(8,128)S(1)}) fusion(pred[2,8,64,1024]{3,2,1,0:T(8,128)(4,1)S(1)} %broadcast_compare_fusion.4, bf16[2,8,1024,128,1]{3,2,4,1,0:T(8,128)(2,1)} %bitcast.138, bf16[1,2,64,2,8,128]{5,4,3,2,1,0:T(8,128)(2,1)S(1)} %constant_dynamic-slice_fusion.4), kind=kOutput, calls=%fused_computation.9.clone.1 | convolution fusion | flops 543160320 | bytes 14163968 | tf_op jit(solution)/shard_map/while/body/eval_jaxpr/tqhgd,tgkd->tghqk/dot_general | solution.py:126
  223.3 5.9 %gather_fusion = bf16[256,64,128]{2,1,0:T(8,128)(2,1)} fusion(bf16[8,40,64,128]{3,2,1,0:T(8,128)(2,1)} %get-tuple-element.210, s32[256]{0:T(256)S(1)} %reshape.360), kind=kCustom, calls=%fused_computation.clone.clone.1 | custom fusion | bytes 8390656 | tf_op jit(solution)/shard_map/while/body/eval_jaxpr/gather | solution.py:119
  229.2 7.3 %fusion.76 = bf16[1,2,64,2,8,128]{5,2,3,4,1,0:T(8,128)(2,1)S(1)} fusion(bf16[2,8,1024,128,1]{3,2,4,1,0:T(8,128)(2,1)} %bitcast.137, f32[2,8,1024,64,2]{2,3,4,1,0:T(8,128)} %copy-done, f32[2,8,2,64]{3,2,1,0:T(2,128)S(1)} %get-tuple-element.188, pred[2,8,64,1024]{3,2,1,0:T(8,128)(4,1)S(1)} %broadcast_compare_fusion.4, f32[2,64,2,8]{1,2,3,0:T(2,128)S(1)} %bitcast.149), kind=kOutput, calls=%fused_computation.18.clone.1 | convolution fusion | flops 545783808 | bytes 14172160 | tf_op jit(solution)/shard_map/while/body/eval_jaxpr/tghqk,tgkd->tqhgd/dot_general | solution.py:133
  238.7 5.8 %gather_fusion.1 = bf16[256,64,128]{2,1,0:T(8,128)(2,1)} fusion(bf16[8,40,64,128]{3,2,1,0:T(8,128)(2,1)} %get-tuple-element.213, s32[256]{0:T(256)S(1)} %reshape.360), kind=kCustom, calls=%fused_computation.1.clone.clone.1 | custom fusion | bytes 8390656 | tf_op jit(solution)/shard_map/while/body/eval_jaxpr/gather | solution.py:116
  251.9 5.9 %gather_fusion = bf16[256,64,128]{2,1,0:T(8,128)(2,1)} fusion(bf16[8,40,64,128]{3,2,1,0:T(8,128)(2,1)} %get-tuple-element.210, s32[256]{0:T(256)S(1)} %reshape.360), kind=kCustom, calls=%fused_computation.clone.clone.1 | custom fusion | bytes 8390656 | tf_op jit(solution)/shard_map/while/body/eval_jaxpr/gather | solution.py:119
  257.8 7.3 %fusion.76 = bf16[1,2,64,2,8,128]{5,2,3,4,1,0:T(8,128)(2,1)S(1)} fusion(bf16[2,8,1024,128,1]{3,2,4,1,0:T(8,128)(2,1)} %bitcast.137, f32[2,8,1024,64,2]{2,3,4,1,0:T(8,128)} %copy-done, f32[2,8,2,64]{3,2,1,0:T(2,128)S(1)} %get-tuple-element.188, pred[2,8,64,1024]{3,2,1,0:T(8,128)(4,1)S(1)} %broadcast_compare_fusion.4, f32[2,64,2,8]{1,2,3,0:T(2,128)S(1)} %bitcast.149), kind=kOutput, calls=%fused_computation.18.clone.1 | convolution fusion | flops 545783808 | bytes 14172160 | tf_op jit(solution)/shard_map/while/body/eval_jaxpr/tghqk,tgkd->tqhgd/dot_general | solution.py:133
  267.3 5.8 %gather_fusion.1 = bf16[256,64,128]{2,1,0:T(8,128)(2,1)} fusion(bf16[8,40,64,128]{3,2,1,0:T(8,128)(2,1)} %get-tuple-element.213, s32[256]{0:T(256)S(1)} %reshape.360), kind=kCustom, calls=%fused_computation.1.clone.clone.1 | custom fusion | bytes 8390656 | tf_op jit(solution)/shard_map/while/body/eval_jaxpr/gather | solution.py:116
  280.4 5.9 %gather_fusion = bf16[256,64,128]{2,1,0:T(8,128)(2,1)} fusion(bf16[8,40,64,128]{3,2,1,0:T(8,128)(2,1)} %get-tuple-element.210, s32[256]{0:T(256)S(1)} %reshape.360), kind=kCustom, calls=%fused_computation.clone.clone.1 | custom fusion | bytes 8390656 | tf_op jit(solution)/shard_map/while/body/eval_jaxpr/gather | solution.py:119
  286.3 7.3 %fusion.76 = bf16[1,2,64,2,8,128]{5,2,3,4,1,0:T(8,128)(2,1)S(1)} fusion(bf16[2,8,1024,128,1]{3,2,4,1,0:T(8,128)(2,1)} %bitcast.137, f32[2,8,1024,64,2]{2,3,4,1,0:T(8,128)} %copy-done, f32[2,8,2,64]{3,2,1,0:T(2,128)S(1)} %get-tuple-element.188, pred[2,8,64,1024]{3,2,1,0:T(8,128)(4,1)S(1)} %broadcast_compare_fusion.4, f32[2,64,2,8]{1,2,3,0:T(2,128)S(1)} %bitcast.149), kind=kOutput, calls=%fused_computation.18.clone.1 | convolution fusion | flops 545783808 | bytes 14172160 | tf_op jit(solution)/shard_map/while/body/eval_jaxpr/tghqk,tgkd->tqhgd/dot_general | solution.py:133
  (126 shorter events, 66.0 us)
Async XLA Ops:
  10.6 17.3 %all-to-all-start.2 = ((s32[2,16,2]{2,0,1:T(2,128)}), s32[2,16,2]{2,0,1:T(2,128)S(1)}, u32[]{:S(2)}, u32[]{:S(2)}) async-start(s32[2,16,2]{2,0,1:T(2,128)} %copy.67), calls=%async_computation.2 | async-start | bytes 32768 | tf_op jit(solution)/shard_map/all_to_all | solution.py:99
  20.5 149.9 %all-gather.2.cloned.1.call-start = ((), (), s32[]{:S(2)}) async-start(), calls=%async_computation.4 | async-start | bytes 10485760 | tf_op jit(solution)/shard_map/all_gather | solution.py:105
  23.3 9.0 %copy-start.2 = (bf16[1,512,8,128]{3,1,2,0:T(8,128)(2,1)}, bf16[1,512,8,128]{3,1,2,0:T(8,128)(2,1)S(1)}, u32[]{:S(2)}) copy-start(bf16[1,512,8,128]{3,1,2,0:T(8,128)(2,1)S(1)} %copy.63) | copy-start | bytes 3145732
  86.4 1.5 copy-start.6
  86.4 5.9 %copy-start.4 = (s32[1,8,8,16]{3,2,1,0:T(8,128)S(1)}, s32[1,8,8,16]{3,2,1,0:T(8,128)}, u32[]{:S(2)}) copy-start(s32[1,8,8,16]{3,2,1,0:T(8,128)} %param.11) | copy-start | bytes 12292
  86.4 16.7 %copy-start.1 = (bf16[1,512,2,8,128]{4,3,2,1,0:T(8,128)(2,1)S(1)}, bf16[1,512,2,8,128]{4,3,2,1,0:T(8,128)(2,1)}, u32[]{:S(2)}) copy-start(bf16[1,512,2,8,128]{4,3,2,1,0:T(8,128)(2,1)} %param.7) | copy-start | bytes 6291460
  88.7 14.4 %all-to-all-start = ((bf16[16,1,8,8,128]{4,2,3,1,0:T(8,128)(2,1)}), bf16[16,1,8,8,128]{4,2,3,1,0:T(8,128)(2,1)S(1)}, u32[]{:S(2)}, u32[]{:S(2)}) async-start(bf16[16,1,8,8,128]{4,2,3,1,0:T(8,128)(2,1)} %broadcast_in_dim.79), calls=%async_computation | async-start | bytes 524288 | tf_op jit(solution)/shard_map/all_to_all | solution.py:20
  106.5 7.6 %copy-start.5 = (pred[512,128]{0,1:T(8,128)(4,1)S(1)}, pred[512,128]{0,1:T(8,128)(4,1)}, u32[]{:S(2)}) copy-start(pred[512,128]{0,1:T(8,128)(4,1)} %iota_compare_fusion.1) | copy-start | bytes 196612
  127.6 8.6 %all-to-all-start.1 = ((bf16[4,1,8,2,128]{4,3,2,1,0:T(2,128)(2,1)}), bf16[4,1,8,2,128]{4,3,2,1,0:T(2,128)(2,1)S(1)}, u32[]{:S(2)}, u32[]{:S(2)}) async-start(bf16[4,1,8,2,128]{4,3,2,1,0:T(2,128)(2,1)} %copy.62), calls=%async_computation.1 | async-start | bytes 32768 | tf_op jit(solution)/shard_map/all_to_all | solution.py:37
  170.5 4.5 %copy-start.3 = (bf16[1,512,8,128]{3,1,2,0:T(8,128)(2,1)S(1)}, bf16[1,512,8,128]{3,1,2,0:T(8,128)(2,1)}, u32[]{:S(2)}) copy-start(bf16[1,512,8,128]{3,1,2,0:T(8,128)(2,1)} %copy-done.2) | copy-start | bytes 3145732
  191.5 3.2 %copy-start = (f32[2,8,1024,64,2]{2,3,4,1,0:T(8,128)}, f32[2,8,1024,64,2]{2,3,4,1,0:T(8,128)S(1)}, u32[]{:S(2)}) copy-start(f32[2,8,1024,64,2]{2,3,4,1,0:T(8,128)S(1)} %get-tuple-element.187) | copy-start | bytes 25165828 | tf_op jit(solution)/shard_map/while
  220.1 3.2 %copy-start = (f32[2,8,1024,64,2]{2,3,4,1,0:T(8,128)}, f32[2,8,1024,64,2]{2,3,4,1,0:T(8,128)S(1)}, u32[]{:S(2)}) copy-start(f32[2,8,1024,64,2]{2,3,4,1,0:T(8,128)S(1)} %get-tuple-element.187) | copy-start | bytes 25165828 | tf_op jit(solution)/shard_map/while
  248.6 3.2 %copy-start = (f32[2,8,1024,64,2]{2,3,4,1,0:T(8,128)}, f32[2,8,1024,64,2]{2,3,4,1,0:T(8,128)S(1)}, u32[]{:S(2)}) copy-start(f32[2,8,1024,64,2]{2,3,4,1,0:T(8,128)S(1)} %get-tuple-element.187) | copy-start | bytes 25165828 | tf_op jit(solution)/shard_map/while
  277.2 3.2 %copy-start = (f32[2,8,1024,64,2]{2,3,4,1,0:T(8,128)}, f32[2,8,1024,64,2]{2,3,4,1,0:T(8,128)S(1)}, u32[]{:S(2)}) copy-start(f32[2,8,1024,64,2]{2,3,4,1,0:T(8,128)S(1)} %get-tuple-element.187) | copy-start | bytes 25165828 | tf_op jit(solution)/shard_map/while
Sparse Core Ops, SparseCore 0:
  88.1 82.3 all-gather.1
where the time goes:
time: 303 us; the launch traced here: 302 us
  local copies, waits for them, and re-layouts  73.2 us (24%)
  blocking collectives  53.9 us (18%)
  waiting for transfers between devices  51.5 us (17%)
  matrix products  48.7 us (16%)
  other arithmetic  42.3 us (14%)
  starting transfers between devices  17.4 us (6%)
  between operations  14.3 us (5%)
    all_to_all x1, blocking collectives, local(): lax.all_to_all(found, 'seq', split_axis=1, concat_axis=1, tiled=True)  53.9 us
    all_gather x1, waiting for transfers between devices, local(): fetched = lax.all_gather(fetched, 'head', axis=0, tiled=True)  33.6 us
    dot_general x4, matrix products, attend(): jnp.einsum('tghqk,tgkd->tqhgd', rounded, value_sel, preferred_element_typ...  29.2 us
    gather x4, local copies, waits for them, and re-layouts, attend(): value_pool[group_sel, index_part]  23.6 us
    gather x4, local copies, waits for them, and re-layouts, attend(): key_pool[group_sel, index_part]  23.2 us
    dot_general x4, matrix products, attend(): jnp.einsum('tqhgd,tgkd->tghqk', query_part, key_sel, preferred_element_ty...  16.2 us
    all_to_all x1, starting transfers between devices, local(): lax.all_to_all(asked_ids, 'seq', split_axis=1, concat_axis=1, tiled=True)  9.97 us
    reduce_sum x4, other arithmetic, softmax_parts(): return (weights, jnp.sum(weights, axis=-1, keepdims=True))  9.72 us
  transfers between devices with their start and end apart: 4, of which 4 were waited for; matrix products, arithmetic and copies ran while one was open for 10% of the time, Pallas kernels for 0%

commit v1 on v0

--- a/solution.py
+++ b/solution.py
@@ -7,6 +7,13 @@
 BLOCK = 64
 TOPN = 16
 CAP = 2
+
+
+def exchange_gather(x, axis, dim):
+    n_dev = lax.axis_size(axis)
+    pieces = jnp.stack([x for _ in range(n_dev)])
+    pieces = lax.all_to_all(pieces, axis, split_axis=0, concat_axis=0)
+    return jnp.concatenate(pieces, axis=dim)
 
 
 def laid_out(blocks, dim):
@@ -102,7 +109,7 @@
         [key_local[requested, :, group_ids, :], value_local[requested, :, group_ids, :]], axis=-1
     )
     fetched = lax.all_to_all(found, "seq", split_axis=1, concat_axis=1, tiled=True)
-    fetched = lax.all_gather(fetched, "head", axis=0, tiled=True)
+    fetched = exchange_gather(fetched, "head", 0)
     key_remote = fetched[..., :head_width].reshape(groups, shards * CAP, block_len, head_width)
     value_remote = fetched[..., head_width:].reshape(groups, shards * CAP, block_len, head_width)
     key_pool = jnp.concatenate([jnp.transpose(key_local, (2, 0, 1, 3)), key_remote], axis=1)

time: 303 us -> 329 us (1.086)
  waiting for transfers between devices: 51.5 us -> 125 us
  blocking collectives: 53.9 us -> 0 us
  between operations: 14.3 us -> 0.88 us
  starting transfers between devices: 17.4 us -> 28 us
  local copies, waits for them, and re-layouts: 73.2 us -> 82 us
    all_to_all x0 -> x2, waiting for transfers between devices: none -> 114 us  [the longest x1 89.4 us: exchange_gather(): pieces = lax.all_to_all(pieces, axis, split_axis=0, concat_axis=0)]
    all_to_all x1 -> x0, blocking collectives: 53.9 us -> none  [local(): lax.all_to_all(found, 'seq', split_axis=1, concat_axis=1, tiled=True)]
    all_gather x1 -> x0, waiting for transfers between devices: 33.6 us -> none  [local(): fetched = lax.all_gather(fetched, 'head', axis=0, tiled=True)]
    all_to_all x0 -> x2, starting transfers between devices: none -> 10.3 us  [the longest x1 5.96 us: exchange_gather(): pieces = lax.all_to_all(pieces, axis, split_axis=0, concat_axis=0)]
    another operation x0 -> x1, local copies, waits for them, and re-layouts: none -> 5.89 us  [exchange_gather(): pieces = jnp.stack([x for _ in range(n_dev)])]
    all_to_all x1, waiting for transfers between devices: 4.56 us -> 1.05 us  [sum_at_owner(): lax.all_to_all(cut_along(value, dim, count), axis, 0, 0, tiled=True)]
  transfers between devices with their start and end apart: 4 -> 5, of which waited for: 4 -> 5; matrix products, arithmetic and copies ran while one was open for 10% -> 12% of each run, Pallas kernels for 0% -> 0%
where the time goes in v1:
time: 329 us; the launch traced here: 326 us
  waiting for transfers between devices  125 us (38%)
  local copies, waits for them, and re-layouts  82 us (25%)
  matrix products  48.7 us (15%)
  other arithmetic  41.2 us (13%)
  starting transfers between devices  28 us (9%)
    all_to_all x1, waiting for transfers between devices, exchange_gather(): pieces = lax.all_to_all(pieces, axis, split_axis=0, concat_axis=0)  89.4 us
    dot_general x4, matrix products, attend(): jnp.einsum('tghqk,tgkd->tqhgd', rounded, value_sel, preferred_element_typ...  29.2 us
    all_to_all x1, waiting for transfers between devices, local(): lax.all_to_all(found, 'seq', split_axis=1, concat_axis=1, tiled=True)  24.2 us
    gather x4, local copies, waits for them, and re-layouts, attend(): value_pool[group_sel, index_part]  23.6 us
    gather x4, local copies, waits for them, and re-layouts, attend(): key_pool[group_sel, index_part]  23.2 us
    dot_general x4, matrix products, attend(): jnp.einsum('tqhgd,tgkd->tghqk', query_part, key_sel, preferred_element_ty...  16.2 us
    all_to_all x1, starting transfers between devices, local(): lax.all_to_all(asked_ids, 'seq', split_axis=1, concat_axis=1, tiled=True)  9.97 us
    reduce_sum x4, other arithmetic, softmax_parts(): return (weights, jnp.sum(weights, axis=-1, keepdims=True))  9.72 us
  transfers between devices with their start and end apart: 5, of which 5 were waited for; matrix products, arithmetic and copies ran while one was open for 12% of the time, Pallas kernels for 0%

profile of v1, /device:TPU:1, one launch (start us, length us, event | category | flops | bytes accessed | tf_op | source)
XLA Modules:
  0.0 326.0 jit_solution(16692509521807975946)
XLA Ops:
  4.0 10.0 %all-to-all-start.2 = ((s32[2,16,2]{2,0,1:T(2,128)}), s32[2,16,2]{2,0,1:T(2,128)S(1)}, u32[]{:S(2)}, u32[]{:S(2)}) async-start(s32[2,16,2]{2,0,1:T(2,128)} %copy.67), calls=%async_computation.2 | async-start | bytes 32768 | tf_op jit(solution)/shard_map/all_to_all | solution.py:106
  16.8 4.6 %all-to-all-done.2 = s32[2,16,2]{2,0,1:T(2,128)S(1)} async-done(((s32[2,16,2]{2,0,1:T(2,128)}), s32[2,16,2]{2,0,1:T(2,128)S(1)}, u32[]{:S(2)}, u32[]{:S(2)}) %all-to-all-start.2) | async-done | bytes 288 | tf_op jit(solution)/shard_map/all_to_all | solution.py:106
  31.8 5.8 %all-to-all-done = bf16[16,1,8,8,128]{4,2,3,1,0:T(8,128)(2,1)S(1)} async-done(((bf16[16,1,8,8,128]{4,2,3,1,0:T(8,128)(2,1)}), bf16[16,1,8,8,128]{4,2,3,1,0:T(8,128)(2,1)S(1)}, u32[]{:S(2)}, u32[]{:S(2)}) %all-to-all-start) | async-done | bytes 262176 | tf_op jit(solution)/shard_map/all_to_all | solution.py:27
  45.3 7.3 %fusion.27 = f32[512,2,8,128]{0,3,1,2:T(8,128)} fusion(f32[8,128,512,2]{2,1,3,0:T(8,128)} %fusion.30, pred[512,128]{0,1:T(8,128)(4,1)S(1)} %iota_compare_fusion.1), kind=kOutput, calls=%fused_computation.35 | output fusion | flops 5259518 | bytes 8454144 | tf_op jit(solution)/shard_map/div | solution.py:77
  52.6 8.0 %divide_reduce_fusion = f32[512,8,128]{0,2,1:T(8,128)} fusion(f32[512,2,8,128]{0,3,1,2:T(8,128)} %fusion.27, f32[8,128,512,2]{2,1,3,0:T(8,128)} %fusion.30, pred[512,128]{0,1:T(8,128)(4,1)S(1)} %iota_compare_fusion.1), kind=kOutput, calls=%fused_computation.40 | output fusion | flops 6824063 | bytes 10551296 | tf_op jit(solution)/shard_map/sub | solution.py:50
  65.9 24.2 %all-to-all-done.3 = bf16[2,16,2,64,256]{4,3,2,0,1:T(8,128)(2,1)} async-done(((bf16[2,16,2,64,256]{4,3,2,0,1:T(8,128)(2,1)}), bf16[2,16,2,64,256]{4,3,2,0,1:T(8,128)(2,1)}, u32[]{:S(2)}, u32[]{:S(2)}) %all-to-all-start.3) | async-done | bytes 2097184 | tf_op jit(solution)/shard_map/all_to_all | solution.py:111
  98.3 5.9 %stack.2 = bf16[4,2,16,2,64,256]{5,4,3,2,1,0:T(8,128)(2,1)} broadcast(bf16[2,16,2,64,256]{4,3,2,1,0:T(8,128)(2,1)} %copy.71), dimensions={1,2,3,4,5} | broadcast | bytes 10485760 | tf_op jit(solution)/shard_map/stack | solution.py:14
  104.2 6.0 %all-to-all-start.4 = ((bf16[4,2,16,2,64,256]{5,4,3,2,1,0:T(8,128)(2,1)}), bf16[4,2,16,2,64,256]{5,4,3,2,1,0:T(8,128)(2,1)}, u32[]{:S(2)}, u32[]{:S(2)}) async-start(bf16[4,2,16,2,64,256]{5,4,3,2,1,0:T(8,128)(2,1)} %stack.2), calls=%async_computation.4 | async-start | bytes 16777216 | tf_op jit(solution)/shard_map/all_to_all | solution.py:15
  112.3 89.4 %all-to-all-done.4 = bf16[4,2,16,2,64,256]{5,4,3,2,1,0:T(8,128)(2,1)} async-done(((bf16[4,2,16,2,64,256]{5,4,3,2,1,0:T(8,128)(2,1)}), bf16[4,2,16,2,64,256]{5,4,3,2,1,0:T(8,128)(2,1)}, u32[]{:S(2)}, u32[]{:S(2)}) %all-to-all-start.4) | async-done | bytes 8388640 | tf_op jit(solution)/shard_map/all_to_all | solution.py:15
  201.7 4.5 %fusion.56 = (bf16[8,16,2,64,128]{4,3,2,1,0:T(8,128)(2,1)S(1)}, bf16[8,16,2,64,128]{4,3,2,1,0:T(8,128)(2,1)S(1)}) fusion(bf16[8,16,2,64,256]{4,3,2,1,0:T(8,128)(2,1)} %bitcast.18), kind=kLoop, calls=%fused_computation.102 | loop fusion | bytes 16777216 | tf_op jit(solution)/shard_map/slice | solution.py:113
  206.3 5.5 %pad_maximum_fusion = (bf16[8,40,64,128]{3,2,1,0:T(8,128)(2,1)}, bf16[8,40,64,128]{3,2,1,0:T(8,128)(2,1)}) fusion(bf16[8,32,64,128]{3,2,1,0:T(8,128)(2,1)S(1)} %bitcast.141, bf16[8,8,64,128]{3,2,1,0:T(8,128)(2,1)S(1)} %bitcast.147, bf16[8,32,64,128]{3,2,1,0:T(8,128)(2,1)S(1)} %bitcast.140, bf16[8,8,64,128]{3,2,1,0:T(8,128)(2,1)S(1)} %bitcast.145), kind=kLoop, calls=%fused_computation.37 | loop fusion | flops 5242880 | bytes 20971520 | tf_op jit(solution)/shard_map/concatenate | solution.py:116
  211.7 114.3 %while.11 = (s32[]{:T(128)}, bf16[4,2,64,2,8,128]{5,4,3,2,1,0:T(8,128)(2,1)}, s32[4,2,8,16]{3,2,1,0:T(8,128)S(1)}, bf16[8,40,64,128]{3,2,1,0:T(8,128)(2,1)}, s32...) while((s32[]{:T(128)}, ...), condition=%wide.region_12.13_spmd.clone, body=%wide.region_9.12_spmd.clone.sunk | while | flops 1098397440 | bytes 91690184 | solution.py:145
  212.9 5.8 %gather_fusion.1 = bf16[256,64,128]{2,1,0:T(8,128)(2,1)} fusion(bf16[8,40,64,128]{3,2,1,0:T(8,128)(2,1)} %get-tuple-element.213, s32[256]{0:T(256)S(1)} %reshape.366), kind=kCustom, calls=%fused_computation.1.clone.clone.1 | custom fusion | bytes 8390656 | tf_op jit(solution)/shard_map/while/body/eval_jaxpr/gather | solution.py:123
  226.0 5.9 %gather_fusion = bf16[256,64,128]{2,1,0:T(8,128)(2,1)} fusion(bf16[8,40,64,128]{3,2,1,0:T(8,128)(2,1)} %get-tuple-element.210, s32[256]{0:T(256)S(1)} %reshape.366), kind=kCustom, calls=%fused_computation.clone.clone.1 | custom fusion | bytes 8390656 | tf_op jit(solution)/shard_map/while/body/eval_jaxpr/gather | solution.py:126
  231.9 7.3 %fusion.76 = bf16[1,2,64,2,8,128]{5,2,3,4,1,0:T(8,128)(2,1)S(1)} fusion(bf16[2,8,1024,128,1]{3,2,4,1,0:T(8,128)(2,1)} %bitcast.138, f32[2,8,1024,64,2]{2,3,4,1,0:T(8,128)} %copy-done, f32[2,8,2,64]{3,2,1,0:T(2,128)S(1)} %get-tuple-element.188, pred[2,8,64,1024]{3,2,1,0:T(8,128)(4,1)S(1)} %broadcast_compare_fusion.4, f32[2,64,2,8]{1,2,3,0:T(2,128)S(1)} %bitcast.150), kind=kOutput, calls=%fused_computation.18.clone.1 | convolution fusion | flops 545783808 | bytes 14172160 | tf_op jit(solution)/shard_map/while/body/eval_jaxpr/tghqk,tgkd->tqhgd/dot_general | solution.py:140
  241.4 5.8 %gather_fusion.1 = bf16[256,64,128]{2,1,0:T(8,128)(2,1)} fusion(bf16[8,40,64,128]{3,2,1,0:T(8,128)(2,1)} %get-tuple-element.213, s32[256]{0:T(256)S(1)} %reshape.366), kind=kCustom, calls=%fused_computation.1.clone.clone.1 | custom fusion | bytes 8390656 | tf_op jit(solution)/shard_map/while/body/eval_jaxpr/gather | solution.py:123
  254.6 5.9 %gather_fusion = bf16[256,64,128]{2,1,0:T(8,128)(2,1)} fusion(bf16[8,40,64,128]{3,2,1,0:T(8,128)(2,1)} %get-tuple-element.210, s32[256]{0:T(256)S(1)} %reshape.366), kind=kCustom, calls=%fused_computation.clone.clone.1 | custom fusion | bytes 8390656 | tf_op jit(solution)/shard_map/while/body/eval_jaxpr/gather | solution.py:126
  260.5 7.3 %fusion.76 = bf16[1,2,64,2,8,128]{5,2,3,4,1,0:T(8,128)(2,1)S(1)} fusion(bf16[2,8,1024,128,1]{3,2,4,1,0:T(8,128)(2,1)} %bitcast.138, f32[2,8,1024,64,2]{2,3,4,1,0:T(8,128)} %copy-done, f32[2,8,2,64]{3,2,1,0:T(2,128)S(1)} %get-tuple-element.188, pred[2,8,64,1024]{3,2,1,0:T(8,128)(4,1)S(1)} %broadcast_compare_fusion.4, f32[2,64,2,8]{1,2,3,0:T(2,128)S(1)} %bitcast.150), kind=kOutput, calls=%fused_computation.18.clone.1 | convolution fusion | flops 545783808 | bytes 14172160 | tf_op jit(solution)/shard_map/while/body/eval_jaxpr/tghqk,tgkd->tqhgd/dot_general | solution.py:140
  270.0 5.8 %gather_fusion.1 = bf16[256,64,128]{2,1,0:T(8,128)(2,1)} fusion(bf16[8,40,64,128]{3,2,1,0:T(8,128)(2,1)} %get-tuple-element.213, s32[256]{0:T(256)S(1)} %reshape.366), kind=kCustom, calls=%fused_computation.1.clone.clone.1 | custom fusion | bytes 8390656 | tf_op jit(solution)/shard_map/while/body/eval_jaxpr/gather | solution.py:123
  283.1 5.9 %gather_fusion = bf16[256,64,128]{2,1,0:T(8,128)(2,1)} fusion(bf16[8,40,64,128]{3,2,1,0:T(8,128)(2,1)} %get-tuple-element.210, s32[256]{0:T(256)S(1)} %reshape.366), kind=kCustom, calls=%fused_computation.clone.clone.1 | custom fusion | bytes 8390656 | tf_op jit(solution)/shard_map/while/body/eval_jaxpr/gather | solution.py:126
  289.0 7.3 %fusion.76 = bf16[1,2,64,2,8,128]{5,2,3,4,1,0:T(8,128)(2,1)S(1)} fusion(bf16[2,8,1024,128,1]{3,2,4,1,0:T(8,128)(2,1)} %bitcast.138, f32[2,8,1024,64,2]{2,3,4,1,0:T(8,128)} %copy-done, f32[2,8,2,64]{3,2,1,0:T(2,128)S(1)} %get-tuple-element.188, pred[2,8,64,1024]{3,2,1,0:T(8,128)(4,1)S(1)} %broadcast_compare_fusion.4, f32[2,64,2,8]{1,2,3,0:T(2,128)S(1)} %bitcast.150), kind=kOutput, calls=%fused_computation.18.clone.1 | convolution fusion | flops 545783808 | bytes 14172160 | tf_op jit(solution)/shard_map/while/body/eval_jaxpr/tghqk,tgkd->tqhgd/dot_general | solution.py:140
  298.6 5.8 %gather_fusion.1 = bf16[256,64,128]{2,1,0:T(8,128)(2,1)} fusion(bf16[8,40,64,128]{3,2,1,0:T(8,128)(2,1)} %get-tuple-element.213, s32[256]{0:T(256)S(1)} %reshape.366), kind=kCustom, calls=%fused_computation.1.clone.clone.1 | custom fusion | bytes 8390656 | tf_op jit(solution)/shard_map/while/body/eval_jaxpr/gather | solution.py:123
  311.7 5.9 %gather_fusion = bf16[256,64,128]{2,1,0:T(8,128)(2,1)} fusion(bf16[8,40,64,128]{3,2,1,0:T(8,128)(2,1)} %get-tuple-element.210, s32[256]{0:T(256)S(1)} %reshape.366), kind=kCustom, calls=%fused_computation.clone.clone.1 | custom fusion | bytes 8390656 | tf_op jit(solution)/shard_map/while/body/eval_jaxpr/gather | solution.py:126
  317.6 7.3 %fusion.76 = bf16[1,2,64,2,8,128]{5,2,3,4,1,0:T(8,128)(2,1)S(1)} fusion(bf16[2,8,1024,128,1]{3,2,4,1,0:T(8,128)(2,1)} %bitcast.138, f32[2,8,1024,64,2]{2,3,4,1,0:T(8,128)} %copy-done, f32[2,8,2,64]{3,2,1,0:T(2,128)S(1)} %get-tuple-element.188, pred[2,8,64,1024]{3,2,1,0:T(8,128)(4,1)S(1)} %broadcast_compare_fusion.4, f32[2,64,2,8]{1,2,3,0:T(2,128)S(1)} %bitcast.150), kind=kOutput, calls=%fused_computation.18.clone.1 | convolution fusion | flops 545783808 | bytes 14172160 | tf_op jit(solution)/shard_map/while/body/eval_jaxpr/tghqk,tgkd->tqhgd/dot_general | solution.py:140
  (125 shorter events, 77.9 us)
Async XLA Ops:
  0.6 16.1 %copy-start.5 = (bf16[1,8,8,128]{3,2,1,0:T(8,128)(2,1)S(1)}, bf16[1,8,8,128]{3,2,1,0:T(8,128)(2,1)}, u32[]{:S(2)}) copy-start(bf16[1,8,8,128]{3,2,1,0:T(8,128)(2,1)} %param.10) | copy-start | bytes 49156
  4.0 17.3 %all-to-all-start.2 = ((s32[2,16,2]{2,0,1:T(2,128)}), s32[2,16,2]{2,0,1:T(2,128)S(1)}, u32[]{:S(2)}, u32[]{:S(2)}) async-start(s32[2,16,2]{2,0,1:T(2,128)} %copy.67), calls=%async_computation.2 | async-start | bytes 32768 | tf_op jit(solution)/shard_map/all_to_all | solution.py:106
  16.8 12.0 %copy-start.2 = (bf16[1,512,8,128]{3,1,2,0:T(8,128)(2,1)}, bf16[1,512,8,128]{3,1,2,0:T(8,128)(2,1)S(1)}, u32[]{:S(2)}) copy-start(bf16[1,512,8,128]{3,1,2,0:T(8,128)(2,1)S(1)} %copy.63) | copy-start | bytes 3145732
  22.1 15.5 %all-to-all-start = ((bf16[16,1,8,8,128]{4,2,3,1,0:T(8,128)(2,1)}), bf16[16,1,8,8,128]{4,2,3,1,0:T(8,128)(2,1)S(1)}, u32[]{:S(2)}, u32[]{:S(2)}) async-start(bf16[16,1,8,8,128]{4,2,3,1,0:T(8,128)(2,1)} %broadcast_in_dim.79), calls=%async_computation | async-start | bytes 524288 | tf_op jit(solution)/shard_map/all_to_all | solution.py:27
  30.3 11.7 %copy-start.1 = (bf16[1,512,2,8,128]{4,3,2,1,0:T(8,128)(2,1)S(1)}, bf16[1,512,2,8,128]{4,3,2,1,0:T(8,128)(2,1)}, u32[]{:S(2)}) copy-start(bf16[1,512,2,8,128]{4,3,2,1,0:T(8,128)(2,1)} %param.7) | copy-start | bytes 6291460
  37.6 52.5 %all-to-all-start.3 = ((bf16[2,16,2,64,256]{4,3,2,0,1:T(8,128)(2,1)}), bf16[2,16,2,64,256]{4,3,2,0,1:T(8,128)(2,1)}, u32[]{:S(2)}, u32[]{:S(2)}) async-start(bf16[2,16,2,64,256]{4,3,2,0,1:T(8,128)(2,1)} %copy.70), calls=%async_computation.3 | async-start | bytes 4194304 | tf_op jit(solution)/shard_map/all_to_all | solution.py:111
  90.0 8.2 %all-to-all-start.1 = ((bf16[4,1,8,2,128]{4,3,2,1,0:T(2,128)(2,1)}), bf16[4,1,8,2,128]{4,3,2,1,0:T(2,128)(2,1)S(1)}, u32[]{:S(2)}, u32[]{:S(2)}) async-start(bf16[4,1,8,2,128]{4,3,2,1,0:T(2,128)(2,1)} %copy.62), calls=%async_computation.1 | async-start | bytes 32768 | tf_op jit(solution)/shard_map/all_to_all | solution.py:44
  104.2 6.2 %copy-start.4 = (s32[1,8,8,16]{3,2,1,0:T(8,128)S(1)}, s32[1,8,8,16]{3,2,1,0:T(8,128)}, u32[]{:S(2)}) copy-start(s32[1,8,8,16]{3,2,1,0:T(8,128)} %param.11) | copy-start | bytes 12292
  104.2 97.6 %all-to-all-start.4 = ((bf16[4,2,16,2,64,256]{5,4,3,2,1,0:T(8,128)(2,1)}), bf16[4,2,16,2,64,256]{5,4,3,2,1,0:T(8,128)(2,1)}, u32[]{:S(2)}, u32[]{:S(2)}) async-start(bf16[4,2,16,2,64,256]{5,4,3,2,1,0:T(8,128)(2,1)} %stack.2), calls=%async_computation.4 | async-start | bytes 16777216 | tf_op jit(solution)/shard_map/all_to_all | solution.py:15
  201.7 4.5 %copy-start.3 = (bf16[1,512,8,128]{3,1,2,0:T(8,128)(2,1)S(1)}, bf16[1,512,8,128]{3,1,2,0:T(8,128)(2,1)}, u32[]{:S(2)}) copy-start(bf16[1,512,8,128]{3,1,2,0:T(8,128)(2,1)} %copy-done.2) | copy-start | bytes 3145732
  222.8 3.2 copy-start
  251.3 3.2 copy-start
  279.9 3.2 copy-start
  308.5 3.2 copy-start
